TPU v7x, 16 devices: a 4x2x1 block of a 4x4x8 slice. The times are simulated.
16 devices in a mesh: dp: 2 (over y, z), cp: 8 (over x, core).
Axes of the slice: x: 4, y: 2, z: 1, core: 2. Of those that a mesh axis runs over, the one named last changes fastest.
The devices are a block of a 4x4x8 slice.
Arguments:
- x_act: bfloat16 [6, 1024, 5120], P('dp', 'cp'), parts along dimension 0
- d_out: bfloat16 [6, 1024, 5120], P('dp', 'cp'), parts along dimension 0
- positions: int32 [6, 1024], P('dp', 'cp'), parts along dimension 0
- ln_gain: float32 [5120], replicated
- ln_bias: float32 [5120], replicated
- w_query: bfloat16 [5120, 32, 128], replicated
- w_key: bfloat16 [5120, 8, 128], replicated
- w_value: bfloat16 [5120, 8, 128], replicated
- w_out: bfloat16 [4096, 5120], replicated
Outputs:
- output 1: bfloat16 [6, 1024, 5120], P('dp', 'cp'), parts along dimension 0
- output 2: bfloat16 [6, 1024, 5120], P('dp', 'cp'), parts along dimension 0
- output 3: float32 [10240, 32, 128], P(('dp', 'cp')), parts along dimension 0
- output 4: float32 [10240, 8, 128], P(('dp', 'cp')), parts along dimension 0
- output 5: float32 [10240, 8, 128], P(('dp', 'cp')), parts along dimension 0
- output 6: float32 [8192, 5120], P(('dp', 'cp')), parts along dimension 0
- output 7: float32 [10240], P('dp'), parts along dimension 0
- output 8: float32 [10240], P('dp'), parts along dimension 0
There are 2 independent parts. A program takes and returns all parts, laid end to end along the dimension named above; an argument that names none is the same for every part.
All inputs are finite; a program needn't handle non-finite values.
Results may differ from a plain program's by a relative error of at most 0.00684726.
Values are sent between devices in bfloat16 or wider.
A program may use at most 768 MiB of HBM per device.

v0:
```python
import math
import jax
import jax.numpy as jnp
from jax import lax
from jax.sharding import PartitionSpec as P

EPS = 1e-5
ROPE_BASE = 10000.0
Q_TILE = 128


def norm_forward(x_act, ln_gain, ln_bias):
    x_f32 = x_act.astype(jnp.float32)
    centered = x_f32 - jnp.mean(x_f32, axis=-1, keepdims=True)
    inv_std = lax.rsqrt(jnp.mean(centered * centered, axis=-1, keepdims=True) + EPS)
    x_hat = centered * inv_std
    return (x_hat * (1.0 + ln_gain) + ln_bias).astype(jnp.bfloat16), x_hat, inv_std


def norm_backward(grad_h, x_hat, inv_std, ln_gain):
    grad_hat = grad_h * (1.0 + ln_gain)
    mean_one = jnp.mean(grad_hat, axis=-1, keepdims=True)
    mean_two = jnp.mean(grad_hat * x_hat, axis=-1, keepdims=True)
    return inv_std * (grad_hat - mean_one - x_hat * mean_two)


def rope_tables(positions, head_dim):
    quarter = head_dim // 4
    freq_tab = jnp.exp(jnp.arange(quarter, dtype=jnp.float32) * (-2.0 * math.log(ROPE_BASE) / (head_dim // 2)))
    angles = positions.astype(jnp.float32)[..., None] * freq_tab
    return jnp.cos(angles)[..., None, :], jnp.sin(angles)[..., None, :]


def rope_rotate(values, cos_tab, sin_tab):
    quarter = cos_tab.shape[-1]
    first_half = values[..., :quarter]
    second_half = values[..., quarter:2 * quarter]
    return jnp.concatenate([first_half * cos_tab - second_half * sin_tab, second_half * cos_tab + first_half * sin_tab, values[..., 2 * quarter:]], axis=-1)


def tile_probs(q_tile, key_all, q_first):
    head_dim = q_tile.shape[-1]
    scores = jnp.einsum('bqkgd,blkd->bkgql', q_tile, key_all, preferred_element_type=jnp.float32) * (head_dim ** -0.5)
    q_index = q_first + jnp.arange(q_tile.shape[1])
    k_index = jnp.arange(key_all.shape[1])
    scores = jnp.where(k_index[None, :] <= q_index[:, None], scores, -1e30)
    shifted = jnp.exp(scores - jnp.max(scores, axis=-1, keepdims=True))
    return shifted / jnp.sum(shifted, axis=-1, keepdims=True)


def attention_forward(q_grouped, key_all, value_all, q_base):
    n_batch, seq_len = q_grouped.shape[0], q_grouped.shape[1]

    def one_tile(tile_idx):
        q_first = tile_idx * Q_TILE
        q_tile = lax.dynamic_slice_in_dim(q_grouped, q_first, Q_TILE, axis=1)
        tile_prob = tile_probs(q_tile, key_all, q_base + q_first)
        tile_mix = jnp.einsum('bkgql,blkd->bqkgd', tile_prob.astype(jnp.bfloat16), value_all, preferred_element_type=jnp.float32)
        return tile_mix.astype(jnp.bfloat16)

    out_tiles = lax.map(one_tile, jnp.arange(seq_len // Q_TILE))
    return jnp.moveaxis(out_tiles, 0, 1).reshape(n_batch * seq_len, -1)


def attention_backward(q_grouped, key_all, value_all, grad_attn, q_base):
    n_batch, seq_len = q_grouped.shape[0], q_grouped.shape[1]
    head_dim = q_grouped.shape[-1]

    def one_tile(acc_pair, tile_idx):
        grad_k, grad_v = acc_pair
        q_first = tile_idx * Q_TILE
        q_tile = lax.dynamic_slice_in_dim(q_grouped, q_first, Q_TILE, axis=1)
        ga_tile = lax.dynamic_slice_in_dim(grad_attn, q_first, Q_TILE, axis=1)
        tile_prob = tile_probs(q_tile, key_all, q_base + q_first)
        grad_prob = jnp.einsum('bqkgd,blkd->bkgql', ga_tile, value_all, preferred_element_type=jnp.float32)
        row_dot = jnp.sum(tile_prob * grad_prob, axis=-1, keepdims=True)
        grad_score = (tile_prob * (grad_prob - row_dot) * (head_dim ** -0.5)).astype(jnp.bfloat16)
        grad_q = jnp.einsum('bkgql,blkd->bqkgd', grad_score, key_all, preferred_element_type=jnp.float32)
        grad_k = grad_k + jnp.einsum('bkgql,bqkgd->blkd', grad_score, q_tile, preferred_element_type=jnp.float32)
        grad_v = grad_v + jnp.einsum('bkgql,bqkgd->blkd', tile_prob.astype(jnp.bfloat16), ga_tile, preferred_element_type=jnp.float32)
        return (grad_k, grad_v), grad_q

    zero_acc = jnp.zeros(key_all.shape, jnp.float32)
    (grad_k, grad_v), q_tiles = lax.scan(one_tile, (zero_acc, zero_acc), jnp.arange(seq_len // Q_TILE))
    grad_q = jnp.moveaxis(q_tiles, 0, 1).reshape(n_batch, seq_len, -1, head_dim)
    return grad_q, grad_k, grad_v


def reduce_rows(values):
    return lax.psum_scatter(values, 'cp', scatter_dimension=0, tiled=True)


def solution(mesh):
    def device_step(x_act, d_out, positions, ln_gain, ln_bias, w_query, w_key, w_value, w_out):
        n_batch, seq_len, n_width = x_act.shape
        q_heads = w_query.shape[1]
        kv_heads, head_dim = w_key.shape[1], w_key.shape[2]
        n_tokens = n_batch * seq_len
        q_base = lax.axis_index('cp') * seq_len
        normed, x_hat, inv_std = norm_forward(x_act, ln_gain, ln_bias)
        flat_h = normed.reshape(n_tokens, n_width)
        cos_tab, sin_tab = rope_tables(positions, head_dim)
        q_act = rope_rotate(jnp.einsum('td,dnh->tnh', flat_h, w_query, preferred_element_type=jnp.float32).reshape(n_batch, seq_len, q_heads, head_dim), cos_tab, sin_tab).astype(jnp.bfloat16)
        k_act = rope_rotate(jnp.einsum('td,dnh->tnh', flat_h, w_key, preferred_element_type=jnp.float32).reshape(n_batch, seq_len, kv_heads, head_dim), cos_tab, sin_tab).astype(jnp.bfloat16)
        v_act = jnp.einsum('td,dnh->tnh', flat_h, w_value, preferred_element_type=jnp.float32).astype(jnp.bfloat16).reshape(n_batch, seq_len, kv_heads, head_dim)
        q_grouped = q_act.reshape(n_batch, seq_len, kv_heads, q_heads // kv_heads, head_dim)
        key_all = lax.all_gather(k_act, 'cp', axis=1, tiled=True)
        value_all = lax.all_gather(v_act, 'cp', axis=1, tiled=True)
        attn_act = attention_forward(q_grouped, key_all, value_all, q_base)
        block_out = (x_act.astype(jnp.float32) + jnp.dot(attn_act, w_out, preferred_element_type=jnp.float32).reshape(n_batch, seq_len, n_width)).astype(jnp.bfloat16)
        grad_flat = d_out.reshape(n_tokens, n_width)
        grad_wo = jnp.einsum('tn,td->nd', attn_act, grad_flat, preferred_element_type=jnp.float32)
        grad_attn = jnp.einsum('td,nd->tn', grad_flat, w_out, preferred_element_type=jnp.float32).astype(jnp.bfloat16).reshape(q_grouped.shape)
        kv_again = lax.all_gather(jnp.stack([k_act, v_act]), 'cp', axis=2, tiled=True)
        grad_q, grad_k_all, grad_v_all = attention_backward(q_grouped, kv_again[0], kv_again[1], grad_attn, q_base)
        grad_k_own = lax.psum_scatter(grad_k_all, 'cp', scatter_dimension=1, tiled=True)
        grad_v_own = lax.psum_scatter(grad_v_all, 'cp', scatter_dimension=1, tiled=True)
        grad_q_pre = rope_rotate(grad_q, cos_tab, -sin_tab).astype(jnp.bfloat16).reshape(n_tokens, q_heads, head_dim)
        grad_k_pre = rope_rotate(grad_k_own, cos_tab, -sin_tab).astype(jnp.bfloat16).reshape(n_tokens, kv_heads, head_dim)
        grad_v_pre = grad_v_own.astype(jnp.bfloat16).reshape(n_tokens, kv_heads, head_dim)
        grad_h = (jnp.einsum('tnh,dnh->td', grad_q_pre, w_query, preferred_element_type=jnp.float32) + jnp.einsum('tnh,dnh->td', grad_k_pre, w_key, preferred_element_type=jnp.float32) + jnp.einsum('tnh,dnh->td', grad_v_pre, w_value, preferred_element_type=jnp.float32)).reshape(n_batch, seq_len, n_width)
        grad_wq = jnp.einsum('td,tnh->dnh', flat_h, grad_q_pre, preferred_element_type=jnp.float32)
        grad_wk = jnp.einsum('td,tnh->dnh', flat_h, grad_k_pre, preferred_element_type=jnp.float32)
        grad_wv = jnp.einsum('td,tnh->dnh', flat_h, grad_v_pre, preferred_element_type=jnp.float32)
        grad_x = (d_out.astype(jnp.float32) + norm_backward(grad_h, x_hat, inv_std, ln_gain)).astype(jnp.bfloat16)
        grad_gain = lax.psum(jnp.sum(grad_h * x_hat, axis=(0, 1)), 'cp')
        grad_bias = lax.psum(jnp.sum(grad_h, axis=(0, 1)), 'cp')
        return (block_out, grad_x, reduce_rows(grad_wq), reduce_rows(grad_wk), reduce_rows(grad_wv), reduce_rows(grad_wo), grad_gain, grad_bias)

    return jax.shard_map(device_step, mesh=mesh, in_specs=(P('dp', 'cp', None), P('dp', 'cp', None), P('dp', 'cp'), P(None), P(None), P(None, None, None), P(None, None, None), P(None, None, None), P(None, None)), out_specs=(P('dp', 'cp', None), P('dp', 'cp', None), P(('dp', 'cp'), None, None), P(('dp', 'cp'), None, None), P(('dp', 'cp'), None, None), P(('dp', 'cp'), None), P('dp'), P('dp')), check_vma=False)
```

profile of v0, /device:TPU:113, one launch (start us, length us, event | category | flops | bytes accessed | tf_op | source)
XLA Modules:
  0.0 1601.7 jit_solution(9652989434098696656)
XLA Ops:
  7.3 2.7 convert_reduce_fusion
  10.0 3.3 fusion.44
  13.4 14.4 copy.96
  27.8 4.2 fusion.37
  32.0 9.7 fusion.24
  41.9 4.2 fusion.78
  50.4 54.4 %copy.97 = bf16[5120,32,128]{0,2,1:T(8,128)(2,1)} copy(bf16[5120,32,128]{2,1,0:T(8,128)(2,1)} %param.14) | data formatting | bytes 83886080 | tf_op args[5]
  104.8 27.5 %fusion.8 = f32[3,128,32,128]{1,3,2,0:T(8,128)S(1)} fusion(bf16[5120,32,128]{0,2,1:T(8,128)(2,1)} %copy.97, bf16[3,128,5120]{2,1,0:T(8,128)(2,1)} %copy-done.6), kind=kOutput, calls=%fused_computation.16 | convolution fusion | flops 16106127360 | bytes 52166656 | tf_op jit(solution)/shard_map/td,dnh->tnh/dot_general | solution.py:103
  133.2 2.7 copy.98
  135.9 2.7 copy.99
  138.6 2.7 copy.100
  141.3 23.1 %convolution_convert_fusion = bf16[384,4096]{1,0:T(8,128)(2,1)} fusion(bf16[384,5120]{1,0:T(8,128)(2,1)} %bitcast.192, bf16[4096,5120]{1,0:T(8,128)(2,1)} %param.17), kind=kOutput, calls=%fused_computation.69 | convolution fusion | flops 16107700224 | bytes 49020928 | tf_op jit(solution)/shard_map/td,nd->tn/dot_general | solution.py:113
  164.4 4.7 reshape.162
  169.1 4.2 copy.125
  173.3 5.3 pad_maximum_fusion
  178.7 21.4 %fusion.54 = f32[3,8,1024,128,4]{3,2,4,1,0:T(8,128)} fusion(bf16[3,128,8,4,128]{4,1,3,2,0:T(8,128)(2,1)S(1)} %pad_maximum_fusion, bf16[2,3,1024,8,128]{2,4,3,1,0:T(8,128)(2,1)} %all-gather.8.cloned.1.call-done), kind=kOutput, calls=%fused_computation.70 | convolution fusion | flops 3221225472 | bytes 59768832 | tf_op jit(solution)/shard_map/while/body/eval_jaxpr/bqkgd,blkd->bkgql/dot_general | solution.py:43
  200.1 53.0 %fusion.107 = (f32[3,8,4,128]{3,2,1,0:T(4,128)S(1)}, f32[3,8,4,128,1024]{3,4,2,1,0:T(8,128)}) fusion(f32[3,8,1024,128,4]{3,2,4,1,0:T(8,128)} %fusion.54, pred[128,1024]{0,1:T(8,128)(4,1)S(1)} %iota_compare_fusion), kind=kOutput, calls=%fused_computation.142 | output fusion | flops 75498496 | bytes 100843520 | tf_op jit(solution)/shard_map/while/body/eval_jaxpr/sub | solution.py:47
  253.2 21.0 %fusion.50 = f32[3,8,1024,128,4]{3,2,4,1,0:T(8,128)} fusion(bf16[3,128,8,4,128]{1,4,3,2,0:T(8,128)(2,1)} %copy.125, bf16[2,3,1024,8,128]{2,4,3,1,0:T(8,128)(2,1)} %all-gather.8.cloned.1.call-done), kind=kOutput, calls=%fused_computation.64 | convolution fusion | flops 3221225472 | bytes 59768832 | tf_op jit(solution)/shard_map/while/body/eval_jaxpr/bqkgd,blkd->bkgql/dot_general | solution.py:75
  274.1 65.5 %fusion.55 = f32[3,1024,8,128]{1,3,2,0:T(8,128)} fusion(bf16[3,128,8,4,128]{4,1,3,2,0:T(8,128)(2,1)S(1)} %pad_maximum_fusion, f32[3,8,1024,128,4]{3,2,4,1,0:T(8,128)} %fusion.50, f32[3,8,4,128,1024]{3,4,2,1,0:T(8,128)} %get-tuple-element.97, f32[3,8,4,128]{3,2,1,0:T(4,128)S(1)} %get-tuple-element.96), kind=kOutput, calls=%fused_computation.71 | convolution fusion | flops 3309319168 | bytes 116441088 | tf_op jit(solution)/shard_map/while/body/eval_jaxpr/bkgql,bqkgd->blkd/dot_general | solution.py:79
  341.5 23.5 %fusion.56 = f32[3,1024,8,128]{1,3,2,0:T(8,128)} fusion(bf16[3,128,8,4,128]{1,4,3,2,0:T(8,128)(2,1)S(1)} %copy-done.3, f32[3,8,4,128,1024]{3,4,2,1,0:T(8,128)} %get-tuple-element.97, f32[3,8,4,128]{3,2,1,0:T(4,128)S(1)} %get-tuple-element.96), kind=kOutput, calls=%fused_computation.72 | convolution fusion | flops 3246391296 | bytes 66109440 | tf_op jit(solution)/shard_map/while/body/eval_jaxpr/bkgql,bqkgd->blkd/dot_general | solution.py:80
  369.1 41.5 %reduce-scatter.9.cloned.1.call-done = f32[3,128,8,128]{1,3,2,0:T(8,128)} async-done(((f32[3,1024,8,128]{1,3,2,0:T(8,128)}), f32[3,128,8,128]{1,3,2,0:T(8,128)}) %reduce-scatter.9.cloned.1.call-update) | async-done | bytes 1572880 | tf_op jit(solution)/shard_map/reduce_scatter | solution.py:116
  414.0 11.6 convolution_bitcast_fusion.2
  426.4 65.0 %fusion.23 = f32[3,8,128,4,128]{4,2,3,1,0:T(8,128)} fusion(f32[3,8,1024,128,4]{3,2,4,1,0:T(8,128)} %fusion.50, bf16[2,3,1024,8,128]{2,4,3,1,0:T(8,128)(2,1)} %all-gather.8.cloned.1.call-done, f32[3,8,4,128,1024]{3,4,2,1,0:T(8,128)} %get-tuple-element.97, f32[3,8,4,128]{3,2,1,0:T(4,128)S(1)} %copy-done.46), kind=kOutput, calls=%fused_computation.32 | convolution fusion | flops 3309319168 | bytes 214007808 | tf_op jit(solution)/shard_map/while/body/eval_jaxpr/bkgql,blkd->bqkgd/dot_general | solution.py:78
  491.4 3.4 slice.96
  494.8 3.6 subtract_convert_fusion
  500.8 11.4 convolution_bitcast_fusion.1
  514.1 32.8 %convolution_bitcast_fusion = f32[5120,32,128]{2,0,1:T(8,128)} fusion(bf16[3,128,5120]{2,1,0:T(8,128)(2,1)} %copy-done.6, bf16[3,128,32,64]{1,3,2,0:T(8,128)(2,1)S(1)} %copy-done.4, bf16[3,128,32,32]{1,3,2,0:T(8,128)(2,1)S(1)} %copy-done.13, bf16[3,128,32,32]{1,3,2,0:T(8,128)(2,1)S(1)} %copy-done.14), kind=kOutput, calls=%fused_computation.13 | convolution fusion | flops 16115564544 | bytes 90963968 | tf_op jit(solution)/shard_map/td,tnh->dnh/dot_general | solution.py:122
  548.8 20.4 %fusion.51 = f32[3,8,1024,128,4]{3,2,4,1,0:T(8,128)} fusion(bf16[3,128,8,4,128]{4,1,3,2,0:T(8,128)(2,1)S(1)} %copy-done.2, bf16[3,1024,8,128]{1,3,2,0:T(8,128)(2,1)} %all-gather.6.cloned.1.call-done), kind=kOutput, calls=%fused_computation.66 | convolution fusion | flops 3221225472 | bytes 59768832 | tf_op jit(solution)/shard_map/while/body/eval_jaxpr/bqkgd,blkd->bkgql/dot_general | solution.py:43
  569.2 53.1 %fusion.106 = (f32[3,8,4,128]{3,2,1,0:T(4,128)S(1)}, f32[3,8,4,128,1024]{3,4,2,1,0:T(8,128)}) fusion(f32[3,8,1024,128,4]{3,2,4,1,0:T(8,128)} %fusion.51, pred[128,1024]{0,1:T(8,128)(4,1)S(1)} %copy-done.37), kind=kOutput, calls=%fused_computation.141 | output fusion | flops 75498496 | bytes 100843520 | tf_op jit(solution)/shard_map/while/body/eval_jaxpr/sub | solution.py:47
  622.4 19.3 %fusion.75 = bf16[3,8,128,4,128]{4,2,3,1,0:T(8,128)(2,1)S(1)} fusion(f32[3,8,4,128,1024]{3,4,2,1,0:T(8,128)} %get-tuple-element.95, f32[3,8,4,128]{3,2,1,0:T(4,128)S(1)} %get-tuple-element.94, bf16[3,1024,8,128]{1,3,2,0:T(8,128)(2,1)} %all-gather.4.cloned.1.call-done), kind=kOutput, calls=%fused_computation.92 | convolution fusion | flops 3247964160 | bytes 59817984 | tf_op jit(solution)/shard_map/while/body/eval_jaxpr/bkgql,blkd->bqkgd/dot_general | solution.py:58
  643.4 4.1 copy.136
  647.5 4.8 reshape_transpose.7
  652.2 33.8 %fusion.108 = f32[4096,5120]{1,0:T(8,128)} fusion(bf16[384,4096]{1,0:T(8,128)(2,1)S(1)} %reshape_transpose.7, bf16[384,5120]{1,0:T(8,128)(2,1)} %bitcast.193), kind=kOutput, calls=%fused_computation.144 | convolution fusion | flops 16106127360 | bytes 90963968 | tf_op jit(solution)/shard_map/tn,td->nd/dot_general | solution.py:112
  687.9 26.0 %fusion.45 = bf16[3,128,5120]{2,1,0:T(8,128)(2,1)} fusion(bf16[3,128,5120]{2,1,0:T(8,128)(2,1)} %param.9, bf16[3,128,4096]{1,2,0:T(8,128)(2,1)S(1)} %bitcast.201, bf16[4096,5120]{1,0:T(8,128)(2,1)} %param.17), kind=kOutput, calls=%fused_computation.59 | convolution fusion | flops 16112025600 | bytes 52953088 | tf_op jit(solution)/shard_map/dot_general | solution.py:110
  713.8 3.9 copy.169
  717.7 3.7 copy.170
  721.4 2.7 copy.171
  724.2 30.9 %fusion.64 = f32[384,5120,1]{1,0,2:T(8,128)} fusion(bf16[5120,32,128]{0,2,1:T(8,128)(2,1)} %copy.97, bf16[384,32,64]{2,0,1:T(8,128)(2,1)} %bitcast.202, bf16[384,32,32]{2,0,1:T(8,128)(2,1)} %bitcast.206, bf16[384,32,32]{2,0,1:T(8,128)(2,1)} %bitcast.205), kind=kOutput, calls=%fused_computation.81 | convolution fusion | flops 16115564544 | bytes 52953088 | tf_op jit(solution)/shard_map/tnh,dnh->td/dot_general | solution.py:121
  757.4 9.6 fusion.81
  767.0 13.5 fusion.105
  780.6 4.7 fusion.43
  785.3 23.8 %all-reduce.1 = (f32[5120]{0:T(1024)}, f32[5120]{0:T(1024)}) all-reduce(f32[5120]{0:T(1024)S(1)} %get-tuple-element.77, f32[5120]{0:T(1024)S(1)} %get-tuple-element.79), channel_id=1, replica_groups=mesh['dp'=2,'cp'=8] {'cp'}, use_global_device_ids=true, to_apply=%region_16.17 | all-reduce | flops 10240 | bytes 81920 | tf_op jit(solution)/shard_map/psum | solution.py:126
  809.1 8.8 fusion.42
  818.0 4.8 copy.138
  822.8 4.8 copy.139
  827.5 362.1 %reduce-scatter.13.cloned.1.call-done = f32[640,32,128]{2,0,1:T(8,128)} async-done(((f32[5120,32,128]{2,0,1:T(8,128)}), f32[640,32,128]{2,0,1:T(8,128)}) %reduce-scatter.13.cloned.1.call-update) | async-done | bytes 10485776 | tf_op jit(solution)/shard_map/reduce_scatter | solution.py:90
  1189.6 14.1 copy.137
  1203.7 391.0 %reduce-scatter.19.cloned.1.call-done = f32[512,5120]{1,0:T(8,128)} async-done(((f32[4096,5120]{1,0:T(8,128)}), f32[512,5120]{1,0:T(8,128)}) %reduce-scatter.19.cloned.1.call-update) | async-done | bytes 10485776
  (151 shorter events, 27.4 us)
Async XLA Ops:
  7.2 6.1 copy-start.43
  7.2 171.5 %all-gather.8.cloned.1.call-start = ((), (), s32[]{:S(2)}) async-start(), calls=%async_computation.8 | async-start | bytes 14155776 | tf_op jit(solution)/shard_map/all_gather | solution.py:114
  10.0 17.8 %copy-start.38 = (f32[3,128]{1,0:T(4,128)}, f32[3,128]{1,0:T(4,128)S(1)}, u32[]{:S(2)}) copy-start(f32[3,128]{1,0:T(4,128)S(1)} %broadcast_multiply_fusion.1) | copy-start | bytes 4612
  13.3 14.4 copy-start.40
  13.3 14.4 copy-start.26
  13.3 14.4 copy-start.44
  13.4 14.4 copy-start.42
  27.8 14.1 slice-start
  32.0 9.9 copy-start.6
  32.0 9.9 slice-start.1
  32.0 9.9 slice-start.2
  41.8 5.6 copy-start.19
  46.1 58.7 %copy-start.9 = (bf16[384,8,128]{2,0,1:T(8,128)(2,1)}, bf16[384,8,128]{2,0,1:T(8,128)(2,1)S(1)}, u32[]{:S(2)}) copy-start(bf16[384,8,128]{2,0,1:T(8,128)(2,1)S(1)} %fusion.78) | copy-start | bytes 2359300
  50.1 360.5 %reduce-scatter.9.cloned.1.call-start = ((), (), s32[]{:S(2)}) async-start(), calls=%async_computation.9 | async-start | bytes 14155776 | tf_op jit(solution)/shard_map/reduce_scatter | solution.py:116
  104.8 27.9 %copy-start.23 = (f32[3,128,32]{1,2,0:T(8,128)S(1)}, f32[3,128,32]{1,2,0:T(8,128)}, u32[]{:S(2)}) copy-start(f32[3,128,32]{1,2,0:T(8,128)} %copy-done.22) | copy-start | bytes 147460
  104.8 27.9 %copy-start.35 = (f32[3,128,32]{1,2,0:T(8,128)S(1)}, f32[3,128,32]{1,2,0:T(8,128)}, u32[]{:S(2)}) copy-start(f32[3,128,32]{1,2,0:T(8,128)} %copy-done.34) | copy-start | bytes 147460
  178.5 95.6 %copy-start.1 = (bf16[3,128,8,4,128]{4,1,3,2,0:T(8,128)(2,1)}, bf16[3,128,8,4,128]{4,1,3,2,0:T(8,128)(2,1)S(1)}, u32[]{:S(2)}) copy-start(bf16[3,128,8,4,128]{4,1,3,2,0:T(8,128)(2,1)S(1)} %pad_maximum_fusion) | copy-start | bytes 9437188
  178.6 21.5 %copy-start.36 = (pred[128,1024]{0,1:T(8,128)(4,1)}, pred[128,1024]{0,1:T(8,128)(4,1)S(1)}, u32[]{:S(2)}) copy-start(pred[128,1024]{0,1:T(8,128)(4,1)S(1)} %iota_compare_fusion) | copy-start | bytes 393220
  253.1 86.6 %copy-start.45 = (f32[3,8,4,128]{3,2,1,0:T(4,128)}, f32[3,8,4,128]{3,2,1,0:T(4,128)S(1)}, u32[]{:S(2)}) copy-start(f32[3,8,4,128]{3,2,1,0:T(4,128)S(1)} %get-tuple-element.96) | copy-start | bytes 147460
  339.6 1.9 copy-start.3
  339.6 158.7 %reduce-scatter.11.cloned.1.call-start = ((), (), s32[]{:S(2)}) async-start(), calls=%async_computation.10 | async-start | bytes 14155776 | tf_op jit(solution)/shard_map/reduce_scatter | solution.py:117
  365.0 1.5 copy-start.18
  365.0 2.6 copy-start.10
  365.0 46.9 %copy-start.24 = (f32[3,128,32]{1,2,0:T(8,128)S(1)}, f32[3,128,32]{1,2,0:T(8,128)}, u32[]{:S(2)}) copy-start(f32[3,128,32]{1,2,0:T(8,128)} %copy-done.22) | copy-start | bytes 147460
  365.0 46.9 %copy-start.32 = (f32[3,128,32]{1,2,0:T(8,128)S(1)}, f32[3,128,32]{1,2,0:T(8,128)}, u32[]{:S(2)}) copy-start(f32[3,128,32]{1,2,0:T(8,128)} %get-tuple-element.91) | copy-start | bytes 147460
  365.0 182.4 %all-gather.6.cloned.1.call-start = ((), (), s32[]{:S(2)}) async-start(), calls=%async_computation.7 | async-start | bytes 7077888 | tf_op jit(solution)/shard_map/all_gather | solution.py:107
  367.5 254.8 %all-gather.4.cloned.1.call-start = ((), (), s32[]{:S(2)}) async-start(), calls=%async_computation.6 | async-start | bytes 7077888 | tf_op jit(solution)/shard_map/all_gather | solution.py:108
  368.8 449.2 %reduce-scatter.15.cloned.1.call-start = ((), (), s32[]{:S(2)}) async-start(), calls=%async_computation.12 | async-start | bytes 23592960 | tf_op jit(solution)/shard_map/reduce_scatter | solution.py:90
  425.7 69.1 %copy-start.25 = (f32[3,128,32]{1,2,0:T(8,128)S(1)}, f32[3,128,32]{1,2,0:T(8,128)}, u32[]{:S(2)}) copy-start(f32[3,128,32]{1,2,0:T(8,128)} %copy-done.22) | copy-start | bytes 147460
  425.7 69.1 %copy-start.33 = (f32[3,128,32]{1,2,0:T(8,128)S(1)}, f32[3,128,32]{1,2,0:T(8,128)}, u32[]{:S(2)}) copy-start(f32[3,128,32]{1,2,0:T(8,128)} %get-tuple-element.91) | copy-start | bytes 147460
  425.7 397.1 %reduce-scatter.17.cloned.1.call-start = ((), (), s32[]{:S(2)}) async-start(), calls=%async_computation.13 | async-start | bytes 23592960 | tf_op jit(solution)/shard_map/reduce_scatter | solution.py:90
  512.2 1.6 copy-start.13
  512.2 1.8 copy-start.14
  512.3 677.3 %reduce-scatter.13.cloned.1.call-start = ((), (), s32[]{:S(2)}) async-start(), calls=%async_computation.11 | async-start | bytes 94371840 | tf_op jit(solution)/shard_map/reduce_scatter | solution.py:90
  546.9 1.9 copy-start.2
  547.0 22.2 %copy-start.37 = (pred[128,1024]{0,1:T(8,128)(4,1)S(1)}, pred[128,1024]{0,1:T(8,128)(4,1)}, u32[]{:S(2)}) copy-start(pred[128,1024]{0,1:T(8,128)(4,1)} %copy-done.36) | copy-start | bytes 393220
  547.0 1047.8 %reduce-scatter.19.cloned.1.call-start = ((), (), s32[]{:S(2)}) async-start(), calls=%async_computation.14 | async-start | bytes 94371840
  641.7 1.7 copy-start.7
  686.0 1.9 copy-start.8
  713.8 7.6 copy-start.5
  724.2 30.9 %copy-start.31 = (bf16[3,128,8,32]{1,3,2,0:T(8,128)(2,1)S(1)}, bf16[3,128,8,32]{1,3,2,0:T(8,128)(2,1)}, u32[]{:S(2)}) copy-start(bf16[3,128,8,32]{1,3,2,0:T(8,128)(2,1)} %copy-done.30) | copy-start | bytes 589828
  724.2 31.3 %copy-start.29 = (bf16[3,128,8,32]{1,3,2,0:T(8,128)(2,1)S(1)}, bf16[3,128,8,32]{1,3,2,0:T(8,128)(2,1)}, u32[]{:S(2)}) copy-start(bf16[3,128,8,32]{1,3,2,0:T(8,128)(2,1)} %copy-done.28) | copy-start | bytes 589828
  724.2 32.5 %copy-start.21 = (bf16[3,128,8,64]{1,3,2,0:T(8,128)(2,1)S(1)}, bf16[3,128,8,64]{1,3,2,0:T(8,128)(2,1)}, u32[]{:S(2)}) copy-start(bf16[3,128,8,64]{1,3,2,0:T(8,128)(2,1)} %copy-done.20) | copy-start | bytes 1179652
  724.2 32.9 %copy-start.12 = (bf16[3,128,8,128]{1,3,2,0:T(8,128)(2,1)S(1)}, bf16[3,128,8,128]{1,3,2,0:T(8,128)(2,1)}, u32[]{:S(2)}) copy-start(bf16[3,128,8,128]{1,3,2,0:T(8,128)(2,1)} %copy-done.11) | copy-start | bytes 2359300
  757.4 9.6 copy-start.27
  767.0 13.6 copy-start
  767.0 13.6 copy-start.39
  767.0 13.6 copy-start.41
  (11 other events, 10.2 us)
Sparse Core Ops, SparseCore 0:
  50.2 70.4 all-gather.7
  339.8 70.8 reduce-scatter.8
  412.9 68.0 reduce-scatter.10
  483.0 40.1 all-gather.5
  524.7 40.5 all-gather.3
  567.5 107.5 reduce-scatter.14
  677.5 107.2 reduce-scatter.16
  787.1 402.4 reduce-scatter.12
  1192.5 402.1 reduce-scatter.18
where the time goes:
time: 1610 us; the launch traced here: 1600 us
  waiting for transfers between devices  795 us (49%)
  matrix products  470 us (29%)
  local copies, waits for them, and re-layouts  151 us (9%)
  other arithmetic  145 us (9%)
  blocking collectives  23.8 us (1%)
    unnamed x10, waiting for transfers between devices  392 us
    reduce_scatter x3, waiting for transfers between devices, reduce_rows(): return lax.psum_scatter(values, 'cp', scatter_dimension=0, tiled=True)  362 us
    sub x2, other arithmetic, tile_probs(): shifted = jnp.exp(scores - jnp.max(scores, axis=-1, keepdims=True))  106 us
    unnamed x105, local copies, waits for them, and re-layouts  104 us
    dot_general x1, matrix products, one_tile(): jnp.einsum('bkgql,bqkgd->blkd', grad_score, q_tile, preferred_element_typ...  65.5 us
    dot_general x1, matrix products, one_tile(): jnp.einsum('bkgql,blkd->bqkgd', grad_score, key_all, preferred_element_ty...  65 us
    dot_general x2, matrix products, tile_probs(): jnp.einsum('bqkgd,blkd->bkgql', q_tile, key_all, preferred_element_type=j...  41.8 us
    reduce_scatter x1, waiting for transfers between devices, device_step(): lax.psum_scatter(grad_k_all, 'cp', scatter_dimension=1, tiled=True)  41.5 us
  transfers between devices with their start and end apart: 9, of which 3 were waited for; matrix products, arithmetic and copies ran while one was open for 34% of the time, Pallas kernels for 0%

commit v1 on v0

v1 whole, which is shorter than its diff:
```python
import functools
import math
import jax
import jax.numpy as jnp
from jax import lax
from jax.experimental import pallas as pl
from jax.experimental.pallas import tpu as pltpu
from jax.sharding import PartitionSpec as P

BF, F32 = jnp.bfloat16, jnp.float32
NT = (((1,), (1,)), ((), ()))
EPS = 1e-5
VL = 67043328
ANY = pl.BlockSpec(memory_space=pl.ANY)
sds = jax.ShapeDtypeStruct
V, DS = pltpu.VMEM, pltpu.SemaphoreType.DMA


def params(**kw): return pltpu.CompilerParams(vmem_limit_bytes=VL, **kw)


def ln_stats(x):
    mean = jnp.mean(x, axis=-1, keepdims=True)
    cen = x - mean
    inv = lax.rsqrt(jnp.mean(cen * cen, axis=-1, keepdims=True) + EPS)
    return cen * inv, inv


def norm_kernel(x_ref, g_ref, c_ref, h_ref):
    x_hat, _ = ln_stats(x_ref[...].astype(F32))
    h_ref[...] = (x_hat * (1.0 + g_ref[...]) + c_ref[...]).astype(BF)


def norm_call(x, gain, bias):
    n, w = x.shape
    bm = n // 6
    row = pl.BlockSpec((1, w), lambda i: (0, 0))
    blk = pl.BlockSpec((bm, w), lambda i: (i, 0))
    return pl.pallas_call(norm_kernel, grid=(n // bm,), in_specs=[blk, row, row], out_specs=blk, out_shape=sds((n, w), BF), compiler_params=params(), name='norm')(x, gain[None], bias[None])


def out_kernel(parts, a_ref, *refs):
    w_refs, (x_ref, o_ref, lhs, sem) = refs[:parts], refs[parts:]
    nb, nk, bt, w4 = a_ref.shape

    @pl.when(pl.program_id(0) == 0)
    def _():
        cps = [pltpu.make_async_copy(a_ref.at[b, n], lhs.at[b * bt:(b + 1) * bt, n * w4:(n + 1) * w4], sem.at[b * nk + n]) for b in range(nb) for n in range(nk)]
        for cp in cps: cp.start()
        for cp in cps: cp.wait()
    kp = w_refs[0].shape[0]
    acc = x_ref[...].astype(F32)
    for k in range(parts): acc += jnp.dot(lhs[:, k * kp:(k + 1) * kp], w_refs[k][...], preferred_element_type=F32)
    o_ref[...] = acc.astype(BF)


def out_call(a_own, w_out, x, tn=512, parts=4):
    nb, nk, bt, w4 = a_own.shape
    k, w = w_out.shape
    m = nb * bt
    wspec = lambda p: pl.BlockSpec((k // parts, tn), lambda i: (p, i))
    return pl.pallas_call(functools.partial(out_kernel, parts), grid=(w // tn,), in_specs=[ANY] + [wspec(p) for p in range(parts)] + [pl.BlockSpec((m, tn), lambda i: (0, i))],
                          out_specs=pl.BlockSpec((m, tn), lambda i: (0, i)), out_shape=sds((m, w), BF), scratch_shapes=[V((m, k), BF), DS((nb * nk,))], compiler_params=params(), name='out')(a_own, *[w_out] * parts, x)


def dwo_kernel(parts, a_ref, *refs):
    dy_refs, (o_ref, lhsT) = refs[:parts], refs[parts:]

    @pl.when(pl.program_id(0) == 0)
    def _(): lhsT[...] = a_ref[...].T
    kp = dy_refs[0].shape[0]
    o_ref[...] = sum(jnp.dot(lhsT[:, k * kp:(k + 1) * kp], dy_refs[k][...], preferred_element_type=F32) for k in range(parts))


def dwo_call(a4, dy, tn=512, parts=3):
    t, m = a4.shape
    w = dy.shape[1]
    spec = lambda p: pl.BlockSpec((t // parts, tn), lambda i: (p, i))
    return pl.pallas_call(functools.partial(dwo_kernel, parts), grid=(w // tn,), in_specs=[pl.BlockSpec((t, m), lambda i: (0, 0))] + [spec(p) for p in range(parts)],
                          out_specs=pl.BlockSpec((m, tn), lambda i: (0, i)), out_shape=sds((m, w), F32), scratch_shapes=[V((m, t), BF)], compiler_params=params(), name='dwo')(a4, *[dy] * parts)


def dw_kernel(nh, h_ref, d_ref, q_ref, k_ref, v_ref, hT, hbuf, rhs, stage, sem):
    nb, nk, seq, dc = d_ref.shape
    me = lax.axis_index('cp')
    i, last = pl.program_id(0), pl.num_programs(0)
    nr = hT.shape[0]
    hd = stage.shape[3]
    per = nh * hd

    def fetch(j, slot, go):
        @pl.when(j < nk // 2)
        def _():
            for b in range(nb):
                for u in range(2):
                    cp = pltpu.make_async_copy(d_ref.at[b, 2 * jnp.minimum(j, nk // 2 - 1) + u, :, 0:per], rhs.at[slot, b * seq:(b + 1) * seq, u * per:(u + 1) * per], sem.at[slot, b * nk + u])
                    cp.start() if go else cp.wait()

        @pl.when(j >= nk // 2)
        def _():
            off = pl.multiple_of(per + (jnp.maximum(j, nk // 2) - nk // 2) * hd, hd)
            for b in range(nb):
                for n in range(nk):
                    cp = pltpu.make_async_copy(d_ref.at[b, n, :, pl.ds(off, hd)], rhs.at[slot, b * seq:(b + 1) * seq, n * hd:(n + 1) * hd], sem.at[slot, b * nk + n])
                    cp.start() if go else cp.wait()

    @pl.when(i == 0)
    def _():
        cp = pltpu.make_async_copy(h_ref.at[:, pl.ds(pl.multiple_of(me * nr, 128), nr)], hbuf, sem.at[2, 0])
        cp.start()
        fetch(0, 0, True)
        cp.wait()
        hT[...] = hbuf[...].T
    slot = i % 2

    @pl.when(i + 1 < last)
    def _(): fetch(i + 1, 1 - slot, True)
    fetch(i, slot, False)
    nq = nk // 2

    def put(j, slot, go):
        def one(ref, n, cond):
            @pl.when(cond)
            def _():
                cp = pltpu.make_async_copy(stage.at[slot], ref.at[:, pl.ds(pl.multiple_of(n * nk, nk), nk), :], sem.at[2, slot + 1])
                cp.start() if go else cp.wait()
        one(q_ref, jnp.minimum(j, nq - 1), j < nq)
        one(k_ref, 0, j == nq)
        one(v_ref, 0, j == nq + 1)

    @pl.when(i >= 2)
    def _(): put(i - 2, slot, False)
    stage[slot] = jnp.dot(hT[...], rhs[slot], preferred_element_type=F32).reshape(stage.shape[1:])
    put(i, slot, True)

    @pl.when(i == last - 1)
    def _():
        put(i - 1, 1 - slot, False)
        put(i, slot, False)


def dw_call(h, d, kv):
    nb, nk, seq, dc = d.shape
    t, w = h.shape
    nr = w // kv
    hd = dc // 6
    nq = nk // 2
    return pl.pallas_call(functools.partial(dw_kernel, 4), grid=(nq + 2,), in_specs=[ANY, ANY], out_specs=[ANY] * 3,
                          out_shape=[sds((nr, nq * nk, hd), F32)] + [sds((nr, nk, hd), F32)] * 2,
                          scratch_shapes=[V((nr, t), BF), V((t, nr), BF), V((2, t, nk * hd), BF), V((2, nr, nk, hd), F32), DS((3, nb * nk))], compiler_params=params(), name='dw')(h, d)


def dh_kernel(nt, parts, d_ref, *refs):
    w_refs, (x_any, dy_any, g_ref, dx_ref, s_ref, lhs, dh, x_ref, dy_ref, sem) = refs[:parts], refs[parts:]
    nb, nk, seq, dc = d_ref.shape
    me = lax.axis_index('cp')
    m = lhs.shape[0]
    bt = m // nb
    i = pl.program_id(0)
    tn = w_refs[0].shape[1]
    late = [pltpu.make_async_copy(x_any, x_ref, sem.at[nb * nk]), pltpu.make_async_copy(dy_any, dy_ref, sem.at[nb * nk + 1])]

    @pl.when(i == 0)
    def _():
        cps = [pltpu.make_async_copy(d_ref.at[b, n, pl.ds(pl.multiple_of(me * bt, bt), bt), :], lhs.at[b * bt:(b + 1) * bt, n * dc:(n + 1) * dc], sem.at[b * nk + n]) for b in range(nb) for n in range(nk)]
        for cp in cps + late: cp.start()
        for cp in cps: cp.wait()

    @pl.when(i < nt)
    def _():
        w = jnp.concatenate([r[k] for r in w_refs for k in range(r.shape[0])], axis=1)
        dh[jnp.minimum(i, nt - 1)] = lax.dot_general(lhs[...], w, NT, preferred_element_type=F32)

    @pl.when(i == nt)
    def _():
        for cp in late: cp.wait()
        s_ref[...] = jnp.zeros_like(s_ref)
        rc = 32
        sub = s_ref.shape[0] // 2
        fold = lambda v: v.reshape(rc // sub, sub, -1).sum(0)

        def body(r, _):
            rr = pl.ds(pl.multiple_of(r * rc, rc), rc)
            x_hat, inv = ln_stats(x_ref[rr, :].astype(F32))
            g = jnp.concatenate([dh[k, rr, :] for k in range(nt)], axis=1)
            gh = g * (1.0 + g_ref[...])
            m1 = jnp.mean(gh, axis=-1, keepdims=True)
            m2 = jnp.mean(gh * x_hat, axis=-1, keepdims=True)
            dx_ref[rr, :] = (dy_ref[rr, :].astype(F32) + inv * (gh - m1 - x_hat * m2)).astype(BF)
            s_ref[0:sub, :] += fold(g * x_hat)
            s_ref[sub:, :] += fold(g)
            return 0
        lax.fori_loop(0, m // rc, body, 0)


def dh_call(d, w2, x, dy, gain, tn=256, parts=3):
    nb, nk, seq, dc = d.shape
    nw, w, tw = w2.shape
    m = x.shape[0]
    nt = w // tn
    wspec = lambda p: pl.BlockSpec((nw // parts, tn, tw), lambda i: (p, jnp.minimum(i, nt - 1), 0))
    return pl.pallas_call(functools.partial(dh_kernel, nt, parts), grid=(nt + 1,), in_specs=[ANY] + [wspec(p) for p in range(parts)] + [ANY, ANY, pl.BlockSpec((1, w), lambda i: (0, 0))],
                          out_specs=[pl.BlockSpec((m, w), lambda i: (0, 0)), pl.BlockSpec((16, w), lambda i: (0, 0))], out_shape=[sds((m, w), BF), sds((16, w), F32)],
                          scratch_shapes=[V((m, nk * dc), BF), V((nt, m, tn), F32), V((m, w), BF), V((m, w), BF), DS((nb * nk + 2,))], compiler_params=params(), name='dh')(d, *[w2] * parts, x, dy, gain[None])


def sum_kernel(ncp, s_ref, o_ref, own, buf, send, recv):
    me = lax.axis_index('cp')
    M = pl.DeviceIdType.MESH
    sub = s_ref.shape[0] // 2
    barrier = pltpu.get_barrier_semaphore()
    for k in range(1, ncp): pl.semaphore_signal(barrier, inc=1, device_id={'cp': (me + k) % ncp}, device_id_type=M)
    for r in (0, 1): own[r:r + 1, :] = jnp.sum(s_ref[r * sub:(r + 1) * sub, :], axis=0, keepdims=True)
    pl.semaphore_wait(barrier, ncp - 1)
    cps = [pltpu.make_async_remote_copy(src_ref=own, dst_ref=buf.at[k], send_sem=send.at[k], recv_sem=recv.at[k], device_id={'cp': (me + k) % ncp}, device_id_type=M) for k in range(1, ncp)]
    for cp in cps: cp.start()
    buf[0] = own[...]
    for cp in cps: cp.wait()
    tot = buf[me]
    for dev in range(1, ncp): tot = tot + buf[(me + ncp - dev) % ncp]
    o_ref[...] = tot


def sum_call(s, ncp, cid):
    full = pl.BlockSpec(memory_space=pltpu.VMEM)
    w = s.shape[1]
    return pl.pallas_call(functools.partial(sum_kernel, ncp), in_specs=[full], out_specs=full, out_shape=sds((2, w), F32),
                          scratch_shapes=[V((2, w), F32), V((ncp, 2, w), F32), DS((ncp,)), DS((ncp,))], compiler_params=pltpu.CompilerParams(collective_id=cid, has_side_effects=True), name='sums')(s)


MASK = -1e30
HD, GQ, QB, HALF = 128, 4, 128, 64
ROT = HALF // 2
QW = GQ * HD
TW = 2 * HD
NCH = 4
UT = 3
SLOTS, RSLOTS = 4, 10
CHUNK = 2
MESH = pl.DeviceIdType.MESH


def rot(x, c, s):
    lane = lax.broadcasted_iota(jnp.int32, x.shape, 1)
    return x * c + jnp.where(lane < ROT, pltpu.roll(x, HD - ROT, 1), pltpu.roll(x, ROT, 1)) * s


def dot(a, b): return jnp.dot(a, b, preferred_element_type=F32)


def ntdot(a, b): return lax.dot_general(a, b, NT, preferred_element_type=F32)


def att_scores(i, q_ref, k_ref, v_ref, da_ref):
    L = QB * (i + 1)
    stack = lambda ref: jnp.concatenate([ref[L - QB:L, HD * h:HD * h + HD] for h in range(GQ)], axis=0)
    q4, da4 = stack(q_ref), stack(da_ref)
    return q4, da4, ntdot(k_ref[0:L, :], q4), ntdot(v_ref[0:L, :], da4)


def att_probs(i, q4, da4, sT, dpT):
    L, scale = QB * (i + 1), HD ** -0.5
    kr = lax.broadcasted_iota(jnp.int32, (QB, GQ * QB), 0)
    qc = lax.broadcasted_iota(jnp.int32, (QB, GQ * QB), 1) & (QB - 1)
    diag = jnp.where(kr <= qc, sT[L - QB:L, :], MASK)
    sT = jnp.concatenate([sT[:L - QB, :], diag], axis=0) if i else diag
    e = jnp.exp2((sT - jnp.max(sT, axis=0, keepdims=True)) * (scale * math.log2(math.e)))
    p = e * (1.0 / jnp.sum(e, axis=0, keepdims=True))
    ds = (p * (dpT - jnp.sum(p * dpT, axis=0, keepdims=True)) * scale).astype(BF)
    return q4, da4, p.astype(BF), ds


def att_store(i, kT, vT, rope, a_ref, d_ref, dk_acc, dv_acc, q4, da4, pb, ds):
    L = QB * (i + 1)
    r, full, head = slice(L - QB, L), slice(0, L), lambda h: slice(HD * h, HD * h + HD)
    aT = dot(vT[:, full], pb)
    for h in range(GQ): a_ref[r, head(h)] = aT[:, head(h)].T.astype(BF)
    dv_acc[full, :] += dot(pb, da4)
    dk_acc[full, :] += dot(ds, q4)
    dqT = dot(kT[:, full], ds)
    c, s = rope[0, r, :], -rope[1, r, :]
    for h in range(GQ): d_ref[r, head(h)] = rot(dqT[:, head(h)].T, c, s).astype(BF)


def kg_kernel(nchip, owned, plan, h_own, dy_own, cs_own, wq, wk, wv, wo,
              h_all, dy_all, w2, a_own, a4, dqkv, cs_all, q_hbm, k_hbm, v_hbm, da_hbm, a_tmp,
              lhs, rope,
              send, recv, csend, crecv, wsend, wrecv, rsend, rrecv, osend, orecv, asend, arecv, fsend, frecv,
              lsem, wsem, osem, isem, iosem, aisem, aosem, ownsem, bsem):
    nb, bt, width = h_own.shape
    nkv = w2.shape[0] // UT
    T = q_hbm.shape[2]
    nloc = nkv // 2
    cb = 2 * bt
    me = lax.axis_index('cp')
    chip, core = me // 2, me % 2
    at = lambda step, c=core: 2 * ((chip + step) % nchip) + c
    right, left, opp, part = at(1), at(nchip - 1), at(2), 2 * chip + 1 - core
    other = 1 - core
    own_t, all_t = (h_own, dy_own), (h_all, dy_all)
    ds = lambda i, n: pl.ds(pl.multiple_of(i * n, n), n)
    blk = lambda a: ds(a, bt)

    barrier = pltpu.get_barrier_semaphore()
    ncp = 2 * nchip
    for k in range(1, ncp): pl.semaphore_signal(barrier, inc=1, device_id={'cp': (me + k) % ncp}, device_id_type=MESH)
    pl.semaphore_wait(barrier, ncp - 1)

    def remote(src, dst, s, r, dev):
        return pltpu.make_async_remote_copy(src_ref=src, dst_ref=dst, send_sem=s, recv_sem=r, device_id={'cp': dev}, device_id_type=MESH)

    local = pltpu.make_async_copy
    pending = []

    def go(make, *ar):
        make(*ar).start()
        pending.append((make, ar))

    def ring(view, own, ss, rs, half):
        def copy(ch, src, slot, dev, lo=0, n=2 * half): return remote(src if src is not None else view(slot, lo, n), view(slot, lo, n), ss.at[ch], rs.at[ch], dev)

        def D():
            for ch, dev in enumerate((right, left, part)): go(copy, ch, own, me, dev)

        def got(ch, slot, lo=0, n=2 * half): copy(ch, None, slot, part, lo, n).wait_recv()

        def Fw():
            got(0, left)
            go(copy, 3, None, left, right, 0, half)
            got(1, right)
            go(copy, 4, None, right, left, half, half)
            go(copy, 5, None, left, part)
            go(copy, 6, None, right, part)

        def G():
            got(3, opp, 0, half)
            got(4, opp, half, half)
            go(copy, 7, None, opp, part)

        def ready(pos):
            if pos == 0: got(2, part)
            if pos == 1: got(6, at(1, other))
            if pos == 2: got(5, at(nchip - 1, other))
            if pos == 3: got(7, at(2, other))
        return D, Fw, G, ready

    rings = []
    for t in range(2 * nb):
        b, kind = t // 2, t % 2
        view = lambda slot, lo, n, b=b, kind=kind: all_t[kind].at[b, pl.ds(pl.multiple_of(slot * bt + lo, bt // 2), n), :]
        rings.append(ring(view, own_t[kind].at[b], send.at[t], recv.at[t], bt // 2))
    oview = lambda slot, lo, n: dqkv.at[owned, slot, pl.ds(lo, n), :]
    rings.append(ring(oview, dqkv.at[owned, me], osend, orecv, q_hbm.shape[2] // 2))

    def cs_copy(b, ch, src, slot, dev): return remote(src, cs_all.at[b, blk(slot), :], csend.at[b, ch], crecv.at[b, ch], dev)

    def cs_send(b):
        for ch, dev in enumerate((right, opp, left, part)): go(cs_copy, b, ch, cs_own.at[b], me, dev)

    def cs_forward(b):
        for ch, slot in enumerate((left, opp, right)):
            cs_copy(b, ch, cs_own.at[b], slot, part).wait_recv()
            go(cs_copy, b, 4 + ch, cs_all.at[b, blk(slot), :], slot, part)

    def cs_ready(b):
        cs_copy(b, 3, cs_own.at[b], part, part).wait_recv()
        for ch, step in enumerate((nchip - 1, 2, 1)): cs_copy(b, 4 + ch, cs_own.at[b], at(step, other), part).wait_recv()

        def scope(cst):
            for dev in range(ncp):
                @pl.when(dev != me)
                def _(): local(cs_all.at[b, dev * bt:(dev + 1) * bt, :], cst.at[dev * bt:(dev + 1) * bt, :], bsem.at[dev]).start()
            local(cs_own.at[b], cst.at[blk(me), :], bsem.at[me]).start()
            for dev in range(ncp): local(cs_own.at[b], cst.at[dev * bt:(dev + 1) * bt, :], bsem.at[dev]).wait()
            packed = cst[...]
            turned = lax.broadcasted_iota(jnp.int32, packed.shape, 1) < HALF
            rope[b, 0] = jnp.where(turned, packed, 1.0)
            rope[b, 1] = jnp.where(turned, pltpu.roll(packed, HALF, 1), 0.0)
        pl.run_scoped(scope, V((T, HD), F32))

    STEP = (0, 1, nchip - 1, 2)
    crow = lambda pos: ds((chip + STEP[pos]) % nchip, cb)

    def loads(t, pos):
        b, kind = t // 2, t % 2
        if pos == 0:
            return [local(own_t[kind].at[b], lhs.at[kind, blk(core), :], lsem.at[kind, 0]), local(all_t[kind].at[b, blk(part), :], lhs.at[kind, blk(other), :], lsem.at[kind, nchip])]
        return [local(all_t[kind].at[b, crow(pos), :], lhs.at[kind, pl.ds(pos * cb, cb), :], lsem.at[kind, pos])]

    def own_back(t): return local(lhs.at[t % 2, blk(core), :], all_t[t % 2].at[t // 2, blk(me), :], ownsem.at[t % 2])

    def load(t, pos_list):
        for pos in pos_list:
            rings[t][3](pos)
            for cp in loads(t, pos): cp.start()

    def key_head(b, i): return me if b == owned else 2 * mine(i // 2) + i % 2

    def tiles(t, pos_list, per, shape, start, wait, compute, dst, mid):
        b, kind = t // 2, t % 2
        m0, m = pos_list[0] * cb, len(pos_list) * cb
        cnt = per * (1 if b == owned else nloc)
        tid = lambda x: per * key_head(b, x // per) + x % per

        def scope(buf, ost):
            for x in range(min(cnt, SLOTS)): start(tid(x), buf, x)
            for pos in pos_list:
                for cp in loads(t, pos): cp.wait()
            if pos_list[0] == 0: own_back(t).start()

            def stores(x, slot, start_it):
                for y, pos in enumerate(pos_list):
                    dst(b, x // per, x % per, crow(pos), ost.at[slot, pl.ds(y * cb, cb), :], slot, y, start_it)

            def body(x, _):
                for when, ops in mid.items():
                    @pl.when(x == when)
                    def _():
                        for op, *ar in ops: ACT[op](*ar)
                slot, ws = x % 2, x % SLOTS
                wait(tid(x), buf, ws)

                @pl.when(x >= 1)
                def _():
                    @pl.when(x + SLOTS - 1 < cnt)
                    def _(): start(tid(x + SLOTS - 1), buf, (x + SLOTS - 1) % SLOTS)

                @pl.when(x >= 2)
                def _(): stores(x - 2, slot, False)
                compute(b, x % per, lambda r, n: lhs[kind, m0 + r:m0 + r + n, :], buf.at[ws], ost, slot, pos_list)
                stores(x, slot, True)
                return 0
            lax.fori_loop(0, cnt, body, 0)
            for x in (cnt - 2, cnt - 1): stores(x, x % 2, False)
            if pos_list[0] == 0: own_back(t).wait()
        pl.run_scoped(scope, V((SLOTS,) + shape, BF), V((2, m, TW), BF))

    def run(cp, start_it): cp.start() if start_it else cp.wait()

    def w_start(n, buf, slot):
        c = width // NCH
        for y in range(NCH): local(w2.at[n, pl.ds(y * c, c), :], buf.at[slot, pl.ds(y * c, c), :], wsem.at[slot]).start()

    def w_wait(n, buf, slot): local(w2.at[n], buf.at[slot], wsem.at[slot]).wait()

    def qkv_dst(b, i, u, rr, src, slot, y, start_it):
        @pl.when(u < 2)
        def _(): run(local(src, q_hbm.at[b, i, rr, ds(jnp.minimum(u, 1), TW)], osem.at[slot, y]), start_it)

        @pl.when(u == 2)
        def _():
            run(local(src.at[:, 0:HD], k_hbm.at[b, i, rr, :], osem.at[slot, y]), start_it)
            run(local(src.at[:, HD:TW], v_hbm.at[b, i, rr, :], osem.at[slot, nchip + y]), start_it)

    def qkv_compute(b, u, left, w, ost, slot, pos_list):
        for y0 in range(0, len(pos_list), CHUNK):
            part_list = pos_list[y0:y0 + CHUNK]
            res = dot(left(y0 * cb, len(part_list) * cb), w[...])
            for y, pos in enumerate(part_list):
                c, s = rope[b, 0, crow(pos), :], rope[b, 1, crow(pos), :]
                rr, ro = slice(y * cb, (y + 1) * cb), slice((y0 + y) * cb, (y0 + y + 1) * cb)
                ost[slot, ro, 0:HD] = rot(res[rr, 0:HD], c, s).astype(BF)
                ost[slot, ro, HD:TW] = jnp.where(u == 2, res[rr, HD:TW], rot(res[rr, HD:TW], c, s)).astype(BF)

    def qkv(b, pos_list, mid={}): tiles(2 * b, pos_list, UT, (width, TW), w_start, w_wait, qkv_compute, qkv_dst, mid)

    def o_start(n, buf, slot):
        c = TW // NCH
        for y in range(NCH): local(wo.at[ds(n * NCH + y, c), :], buf.at[slot, pl.ds(y * c, c), :], wsem.at[slot]).start()

    def o_wait(n, buf, slot): local(wo.at[ds(n, TW), :], buf.at[slot], wsem.at[slot]).wait()

    def da_dst(b, i, u, rr, src, slot, y, start_it): run(local(src, da_hbm.at[b, i, rr, ds(u, TW)], osem.at[slot, y]), start_it)

    def da_compute(b, u, left, w, ost, slot, pos_list):
        for y0 in range(0, len(pos_list), CHUNK):
            n = min(CHUNK, len(pos_list) - y0) * cb
            ost[slot, y0 * cb:y0 * cb + n, :] = ntdot(left(y0 * cb, n), w[...]).astype(BF)

    def da(b, pos_list, mid={}): tiles(2 * b + 1, pos_list, 2, (TW, width), o_start, o_wait, da_compute, da_dst, mid)

    OCT = nkv

    def rl(src_of, dst_of, nblk):
        def scope(wst, wrl):
            for i in range(RSLOTS): src_of(i, wst.at[i], i).start()

            def body(j, _):
                for u in range(RSLOTS):
                    i, slot = RSLOTS * j + u, u % 2
                    src_of(i, wst.at[u], u).wait()

                    @pl.when(i >= 2)
                    def _():
                        for cp in dst_of(i - 2, wrl.at[slot], slot): cp.wait()
                    wrl[slot] = wst[u].reshape(RB, OCT * HD)
                    for cp in dst_of(i, wrl.at[slot], slot): cp.start()

                    @pl.when(i + RSLOTS < nblk)
                    def _(): src_of(i + RSLOTS, wst.at[u], u).start()
                return 0
            lax.fori_loop(0, nblk // RSLOTS, body, 0)
            for slot in (0, 1):
                for cp in dst_of(nblk - 2 + slot, wrl.at[slot], slot): cp.wait()
        pl.run_scoped(scope, V((RSLOTS, RB, OCT, HD), BF), V((2, RB, OCT * HD), BF))

    half_w = width // 2
    mine = lambda t: t * 2 + core
    theirs = lambda t: t * 2 + other

    def q_tile(octet, x): return UT * (2 * octet + x // 2) + x % 2

    def w_copy(ch, tile, rows): return remote(w2.at[tile, rows, :], w2.at[tile, rows, :], wsend.at[ch], wrecv.at[ch], part)

    def rl_q(t):
        rl(lambda i, buf, slot: local(wq.at[ds(i, RB), ds(mine(t), OCT), :], buf, isem.at[slot]),
           lambda i, buf, slot: [local(buf.at[:, pl.ds(TW * x, TW)], w2.at[q_tile(mine(t), x), ds(i, RB), :], iosem.at[slot, x]) for x in range(NCH)], width // RB)

    def q_copy(t, x): return w_copy(t * NCH + x, q_tile(mine(t), x), pl.ds(0, width))

    def q_send(t):
        for x in range(NCH): go(q_copy, t, x)

    def rl_kv(kv):
        w = (wk, wv)[kv]
        base = half_w // RB
        rl(lambda i, buf, slot: local(w.at[ds(core * base + i, RB)], buf, isem.at[slot]),
           lambda i, buf, slot: [local(buf.at[:, pl.ds(n * HD, HD)], w2.at[UT * n + 2, ds(core * base + i, RB), kv * HD:(kv + 1) * HD], iosem.at[slot, n]) for n in range(nkv)], base)
        if kv:
            for n in range(nkv): go(w_copy, 2 * NCH + n, UT * n + 2, ds(core, half_w))

    def wq_ready():
        for t in (0, 1):
            for x in range(NCH): w_copy(t * NCH + x, q_tile(theirs(t), x), pl.ds(0, width)).wait_recv()

    def wkv_ready():
        for n in range(nkv): w_copy(2 * NCH + n, UT * n + 2, ds(other, half_w)).wait_recv()

    def att_ins(b, i, slot, bufs): return [local(src.at[b, i], dst.at[slot], aisem.at[slot, x]) for x, (src, dst) in enumerate(zip((q_hbm, k_hbm, v_hbm, da_hbm), bufs))]

    def att_outs(b, i, slot, out_a, out_d):
        n = key_head(b, i)
        return [local(out_a.at[slot], a_tmp.at[b, i], aosem.at[slot, 0]), local(out_d.at[slot], dqkv.at[b, n], aosem.at[slot, 1]), local(out_a.at[slot, blk(me), :], a_own.at[b, n], aosem.at[slot, 2])]

    def keep(b, i, slot, out_a, start_it):
        @pl.when(key_head(b, i) == me)
        def _(): run(local(out_a.at[slot], a4.at[b], aosem.at[slot, 3]), start_it)

    whole = [b for b in range(nb) if b != owned]

    def pair_copies(b, i, n):
        f = whole.index(b)
        return [remote(dqkv.at[b, n], dqkv.at[b, n], rsend.at[f, i, 0], rrecv.at[f, i, 0], part),
                remote(a_tmp.at[b, i, blk(part), :], a_own.at[b, n], rsend.at[f, i, 1], rrecv.at[f, i, 1], part)]

    def four_copy(b, i): return remote(a_tmp.at[b, i], a4.at[b], fsend.at[whole.index(b)], frecv.at[whole.index(b)], part)

    def att(b):
        cnt = 1 if b == owned else nloc

        def scope(in_q, in_k, in_v, in_da, out_a, out_d, dk_acc, dv_acc, kT, vT):
            bufs = (in_q, in_k, in_v, in_da)
            for cp in att_ins(b, 0, 0, bufs): cp.start()

            def done(i, slot):
                for cp in att_outs(b, i, slot, out_a, out_d): cp.wait()
                keep(b, i, slot, out_a, False)
                if b != owned:
                    for cp in pair_copies(b, i, key_head(b, i)): cp.start()

                    @pl.when(key_head(b, i) == part)
                    def _(): four_copy(b, i).start()

            def body(i, _):
                slot = i % 2
                for cp in att_ins(b, i, slot, bufs): cp.wait()

                @pl.when(i + 1 < cnt)
                def _():
                    for cp in att_ins(b, i + 1, 1 - slot, bufs): cp.start()

                @pl.when(i >= 2)
                def _(): done(i - 2, slot)
                hook(b, i)
                q, k, v, g = (r.at[slot] for r in bufs)
                dk_acc[...] = jnp.zeros_like(dk_acc)
                dv_acc[...] = jnp.zeros_like(dv_acc)
                kT[...] = k[...].T
                vT[...] = v[...].T
                nblk = T // QB
                scores = att_scores(0, q, k, v, g)
                for x in range(nblk):
                    following = att_scores(x + 1, q, k, v, g) if x + 1 < nblk else None
                    att_store(x, kT, vT, rope.at[b], out_a.at[slot], out_d.at[slot], dk_acc, dv_acc, *att_probs(x, *scores))
                    scores = following
                out_d[slot, :, QW:QW + HD] = rot(dk_acc[...], rope[b, 0], -rope[b, 1]).astype(BF)
                out_d[slot, :, QW + HD:] = dv_acc[...].astype(BF)
                for cp in att_outs(b, i, slot, out_a, out_d): cp.start()
                keep(b, i, slot, out_a, True)
                return 0
            lax.fori_loop(0, cnt, body, 0)
            for i in range(max(cnt - 2, 0), cnt): done(i, i % 2)
        two = lambda w: V((2, T, w), BF)
        pl.run_scoped(scope, two(QW), two(HD), two(HD), two(QW), two(QW), two(QW + TW), V((T, HD), F32), V((T, HD), F32), V((HD, T), BF), V((HD, T), BF))

    hooks = {}

    def hook(b, i):
        for j, ops in hooks.get(b, {}).items():
            @pl.when(i == j)
            def _():
                for op, *ar in ops: ACT[op](*ar)

    def a_copy(k, src, slot, dev): return remote(src, a_own.at[owned, slot], asend.at[k], arecv.at[k], dev)

    def a_send():
        for k in range(1, ncp): go(a_copy, k, a_tmp.at[owned, 0, blk((me + k) % ncp), :], me, (me + k) % ncp)

    def all_in():
        for k in range(1, ncp): a_copy(k, a_tmp.at[owned, 0, blk(me), :], (me + ncp - k) % ncp, part).wait_recv()
        for b in whole:
            for i in range(nloc):
                for cp in pair_copies(b, i, key_head(b, i)): cp.wait_send()
                for cp in pair_copies(b, i, 2 * theirs(i // 2) + i % 2): cp.wait_recv()

            @pl.when(chip % 2 == core)
            def _(): four_copy(b, 0).wait_send()

            @pl.when(chip % 2 != core)
            def _(): four_copy(b, 0).wait_recv()

    ACT = {'L0': lambda t, ps: [cp.start() for p in ps for cp in loads(t, p)], 'T': cs_send, 'TF': cs_forward, 'TR': cs_ready, 'D': lambda t: rings[t][0](), 'F': lambda t: rings[t][1](), 'G': lambda t: rings[t][2](), 'N': lambda t, ps: [rings[t][3](p) for p in ps],
           'L': load, 'RQ': rl_q, 'SQ': q_send, 'RK': rl_kv, 'WQ': wq_ready, 'WK': wkv_ready, 'Q': qkv, 'O': da, 'AS': a_send, 'IN': all_in, 'H': lambda b, j, ops: hooks.setdefault(b, {}).update({j: ops}), 'A': att}
    for op, *ar in plan: ACT[op](*ar)
    for make, ar in pending: make(*ar).wait_send()


S0, S1, S2, S3, S4, S5, S6, S7, S8, S9, S10 = range(11)
NEAR, FAR, EACH, HERE, AWAY = (S0, S1, S2), (S3,), (S0, S1, S2, S3), (S0,), (S1, S2, S3)
PLAN = [('T', S0), ('D', S0), ('D', S1), ('T', S1), ('T', S2), ('RK', S0), ('RK', S1), ('RQ', S0), ('TF', S0), ('F', S0), ('D', S2), ('RQ', S1), ('TR', S0), ('L', S0, NEAR), ('WK',),
        ('Q', S0, NEAR, {S2: [('SQ', S0)], S6: [('F', S1), ('D', S3)], S10: [('L', S1, NEAR)]}), ('G', S0), ('L', S0, FAR), ('SQ', S1), ('O', S0, NEAR), ('TF', S1), ('TF', S2), ('Q', S0, FAR),
        ('F', S2), ('D', S4), ('G', S1), ('L', S1, FAR), ('TR', S1), ('TR', S2), ('L', S2, NEAR), ('O', S0, FAR),
        ('H', S0, S1, [('F', S3), ('D', S5)]), ('H', S0, S2, [('L', S3, NEAR), ('G', S2), ('L', S2, FAR)]), ('A', S0), ('WQ',),
        ('Q', S1, EACH), ('L', S4, HERE), ('F', S4), ('Q', S2, HERE), ('G', S3), ('L', S3, FAR), ('L', S4, NEAR[S1:]), ('O', S1, EACH), ('L', S5, HERE), ('A', S1),
        ('F', S5), ('D', S6), ('AS',), ('G', S4), ('L', S4, FAR), ('L', S5, NEAR[S1:]), ('Q', S2, AWAY, {S9: [('G', S5), ('L', S5, FAR)]}), ('O', S2, EACH), ('H', S2, S1, [('F', S6)]), ('H', S2, S3, [('G', S6)]), ('A', S2), ('N', S6, EACH), ('IN',)]
RB = 128


def kg_call(h_own, dy_own, cs_own, wq, wk, wv, wo, ncp, owned=1, plan=None):
    nb, bt, width = h_own.shape
    T = bt * ncp
    nkv = wk.shape[1]
    nloc = nkv // 2
    seqs = lambda *s: sds((nb,) + s, BF)
    outs = [seqs(T, width)] * 2 + [sds((UT * nkv, width, TW), BF), seqs(nkv, bt, QW), seqs(T, QW), seqs(nkv, T, QW + TW), sds((nb, T, HD), F32),
            seqs(nloc, T, QW), seqs(nloc, T, HD), seqs(nloc, T, HD), seqs(nloc, T, QW), seqs(nloc, T, QW)]
    two = lambda *s: [DS(s), DS(s)]
    scratch = [V((2, T, width), BF), V((nb, 2, T, HD), F32)] + two(2 * nb, 8) + two(nb, 7) + two(2 * NCH + nkv) + two(nb - 1, nloc, 2) + two(8) + two(ncp) + two(nb - 1)
    scratch += [DS((2, 5)), DS((SLOTS,)), DS((2, 8)), DS((RSLOTS,)), DS((2, 8)), DS((2, 4)), DS((2, 4)), DS((2,)), DS((ncp,))]
    return pl.pallas_call(functools.partial(kg_kernel, ncp // 2, owned, plan or PLAN), out_shape=outs, in_specs=[ANY] * 7, out_specs=[ANY] * len(outs), scratch_shapes=scratch,
                          compiler_params=params(collective_id=0, has_side_effects=True), name='gather')(h_own, dy_own, cs_own, wq, wk, wv, wo)


ROPE_BASE = 10000.0


def rope_table(positions):
    freq_tab = jnp.exp(jnp.arange(ROT, dtype=F32) * (-2.0 * math.log(ROPE_BASE) / HALF))
    angles = positions.astype(F32)[..., None] * freq_tab
    cos, sin = jnp.cos(angles), jnp.sin(angles)
    return jnp.concatenate([cos, cos, -sin, sin], -1)


def solution(mesh):
    ncp = mesh.shape['cp']

    def device_step(x_act, d_out, positions, ln_gain, ln_bias, w_query, w_key, w_value, w_out):
        nb, bt, width = x_act.shape
        flat = lambda v: v.reshape(nb * v.shape[1], v.shape[2])
        x, dy = flat(x_act), flat(d_out)
        h = norm_call(x, ln_gain, ln_bias).reshape(x_act.shape)
        h_all, dy_all, w2, a_own, a4, dqkv = kg_call(h, d_out, rope_table(positions), w_query, w_key, w_value, w_out, ncp)[:6]
        dx, sums = dh_call(dqkv, w2, x, dy, ln_gain)
        sums = sum_call(sums, ncp, 1)
        block_out = out_call(a_own, w_out, x)
        dwo = dwo_call(flat(a4), flat(dy_all))
        dwq, dwk, dwv = dw_call(flat(h_all), dqkv, ncp)
        return (block_out.reshape(x_act.shape), dx.reshape(x_act.shape), dwq, dwk, dwv, dwo, sums[0], sums[1])

    row, rep = P('dp', 'cp', None), P(None)
    wrow = P(('dp', 'cp'), None, None)
    return jax.shard_map(device_step, mesh=mesh, in_specs=(row, row, P('dp', 'cp'), rep, rep, rep, rep, rep, rep),
                         out_specs=(row, row, wrow, wrow, wrow, P(('dp', 'cp'), None), P('dp'), P('dp')), check_vma=False)
```

time: 1610 us -> 558 us (0.35)
  waiting for transfers between devices: 795 us -> 0 us
  Pallas kernels: 0 us -> 543 us
  matrix products: 470 us -> 0 us
  local copies, waits for them, and re-layouts: 151 us -> 1.5 us
  other arithmetic: 145 us -> 2.36 us
  blocking collectives: 23.8 us -> 0 us
    pallas_call x0 -> x7, Pallas kernels: none -> 543 us  [the longest x1 390 us: kg_call(): pl.pallas_call(functools.partial(kg_kernel, ncp // 2, owned, plan or PLAN...]
    dot_general x19 -> x0, matrix products: 470 us -> none  [the longest x1 65.5 us: one_tile(): jnp.einsum('bkgql,bqkgd->blkd', grad_score, q_tile, preferred_element_typ...]
    reduce_scatter x5 -> x0, waiting for transfers between devices: 404 us -> none  [the longest x3 362 us: reduce_rows(): return lax.psum_scatter(values, 'cp', scatter_dimension=0, tiled=True)]
    unnamed x10 -> x0, waiting for transfers between devices: 392 us -> none
    sub x2 -> x0, other arithmetic: 106 us -> none  [tile_probs(): shifted = jnp.exp(scores - jnp.max(scores, axis=-1, keepdims=True))]
    unnamed x105 -> x0, local copies, waits for them, and re-layouts: 104 us -> none
    psum x1 -> x0, blocking collectives: 23.8 us -> none  [device_step(): grad_gain = lax.psum(jnp.sum(grad_h * x_hat, axis=(0, 1)), 'cp')]
    concatenate x10 -> x0, local copies, waits for them, and re-layouts: 20.4 us -> none  [rope_rotate(): jnp.concatenate([first_half * cos_tab - second_half * sin_tab, second_hal...]
  transfers between devices with their start and end apart: 9 -> 0, of which waited for: 3 -> 0; matrix products, arithmetic and copies ran while one was open for 34% -> 0% of each run, Pallas kernels for 0% -> 0%
where the time goes in v1:
time: 558 us; the launch traced here: 548 us
  Pallas kernels  543 us (97%)
    pallas_call x1, Pallas kernels, kg_call(): pl.pallas_call(functools.partial(kg_kernel, ncp // 2, owned, plan or PLAN...  390 us
    pallas_call x1, Pallas kernels, dh_call(): pl.pallas_call(functools.partial(dh_kernel, nt, parts), grid=(nt + 1,), i...  50.1 us
    pallas_call x1, Pallas kernels, dw_call(): pl.pallas_call(functools.partial(dw_kernel, 4), grid=(nq + 2,), in_specs=...  32.3 us
    pallas_call x1, Pallas kernels, out_call(): pl.pallas_call(functools.partial(out_kernel, parts), grid=(w // tn,), in_...  26.7 us
    pallas_call x1, Pallas kernels, dwo_call(): pl.pallas_call(functools.partial(dwo_kernel, parts), grid=(w // tn,), in_...  25.2 us

profile of v1, /device:TPU:113, one launch (start us, length us, event | category | flops | bytes accessed | tf_op | source)
XLA Modules:
  0.0 547.7 jit_solution(9676337681499676251)
XLA Ops:
  0.6 0.7 convert_element_type.3
  1.3 0.8 multiply_cosine_fusion
  2.1 0.9 pad_maximum_fusion.cs_own
  3.0 7.4 %norm.1 = bf16[384,5120]{1,0:T(8,128)(2,1)} custom-call(bf16[384,5120]{1,0:T(8,128)(2,1)} %bitcast.15, f32[1,5120]{1,0:T(1,128)} %bitcast.23, f32[1,5120]{1,0:T(1,128)} %bitcast.25), custom_call_target="tpu_custom_call" | custom-call | tf_op jit(solution)/shard_map/norm/pallas_call | solution.py:39
  10.4 390.1 %gather.1 = (bf16[3,1024,5120]{2,1,0:T(8,128)(2,1)}, bf16[3,1024,5120]{2,1,0:T(8,128)(2,1)}, bf16[24,5120,256]{2,1,0:T(8,128)(2,1)}, bf16[3,8,128,512]{3,2,1,0:T...) custom-call(bf16[3,128,5120]{2,1,0:T(8,128)(2,1)} %bitcast.19, ...), custom_call_target="tpu_custom_call" | custom-call | tf_op jit(solution)/shard_map/gather/pallas_call | solution.py:660
  400.4 26.7 %out.1 = bf16[384,5120]{1,0:T(8,128)(2,1)} custom-call(bf16[3,8,128,512]{3,2,1,0:T(8,128)(2,1)} %get-tuple-element.19.a_ref, bf16[4096,5120]{1,0:T(8,128)(2,1)} %refs_3_.1, bf16[4096,5120]{1,0:T(8,128)(2,1)} %refs_3_.1, bf16[4096,5120]{1,0:T(8,128)(2,1)} %refs_3_.1, bf16[4096,5120]{1,0:T(8,128)(2,1)} %refs_3_.1, bf16[384,5120]{1,0:T(8,128)(2,1)} %bitcast.16), custom_call_target="tpu_custom_call" | custom-call | tf_op jit(solution)/shard_map/out/pallas_call | solution.py:62
  427.1 50.1 %dh.1 = (bf16[384,5120]{1,0:T(8,128)(2,1)}, f32[16,5120]{1,0:T(8,128)}) custom-call(bf16[3,8,1024,768]{3,2,1,0:T(8,128)(2,1)} %get-tuple-element.20.d_ref, bf16[24,5120,256]{2,1,0:T(8,128)(2,1)} %get-tuple-element.21.refs_0_.refs_1_.refs_2_, bf16[24,5120,256]{2,1,0:T(8,128)(2,1)} %get-tuple-element.21.refs_0_.refs_1_.refs_2_, ...), custom_call_target="tpu_custom_call" | custom-call | tf_op jit(solution)/shard_map/dh/pallas_call | solution.py:202
  477.3 32.3 %dw.1 = (f32[640,32,128]{2,1,0:T(8,128)}, f32[640,8,128]{2,1,0:T(8,128)}, f32[640,8,128]{2,1,0:T(8,128)}) custom-call(bf16[3072,5120]{1,0:T(8,128)(2,1)} %bitcast.18, bf16[3,8,1024,768]{3,2,1,0:T(8,128)(2,1)} %get-tuple-element.20.d_ref), custom_call_target="tpu_custom_call" | custom-call | tf_op jit(solution)/shard_map/dw/pallas_call | solution.py:148
  509.5 11.0 %sums.1 = f32[2,5120]{1,0:T(2,128)} custom-call(f32[16,5120]{1,0:T(8,128)} %get-tuple-element.29.s_ref), custom_call_target="tpu_custom_call" | custom-call | tf_op jit(solution)/shard_map/sums/pallas_call | solution.py:227
  520.5 1.5 fusion.1
  522.0 25.2 %dwo.1 = f32[512,5120]{1,0:T(8,128)} custom-call(bf16[3072,512]{1,0:T(8,128)(2,1)} %bitcast.22, bf16[3072,5120]{1,0:T(8,128)(2,1)} %bitcast.12, bf16[3072,5120]{1,0:T(8,128)(2,1)} %bitcast.13, bf16[3072,5120]{1,0:T(8,128)(2,1)} %bitcast.14), custom_call_target="tpu_custom_call" | custom-call | tf_op jit(solution)/shard_map/dwo/pallas_call | solution.py:79
  (1 shorter events, 0.0 us)

commit v2 on v1

--- a/solution.py
+++ b/solution.py
@@ -33,7 +33,7 @@
 
 def norm_call(x, gain, bias):
     n, w = x.shape
-    bm = n // 6
+    bm = n // 3
     row = pl.BlockSpec((1, w), lambda i: (0, 0))
     blk = pl.BlockSpec((bm, w), lambda i: (i, 0))
     return pl.pallas_call(norm_kernel, grid=(n // bm,), in_specs=[blk, row, row], out_specs=blk, out_shape=sds((n, w), BF), compiler_params=params(), name='norm')(x, gain[None], bias[None])
@@ -72,7 +72,7 @@
     o_ref[...] = sum(jnp.dot(lhsT[:, k * kp:(k + 1) * kp], dy_refs[k][...], preferred_element_type=F32) for k in range(parts))
 
 
-def dwo_call(a4, dy, tn=512, parts=3):
+def dwo_call(a4, dy, tn=1024, parts=3):
     t, m = a4.shape
     w = dy.shape[1]
     spec = lambda p: pl.BlockSpec((t // parts, tn), lambda i: (p, i))
@@ -193,7 +193,7 @@
         lax.fori_loop(0, m // rc, body, 0)
 
 
-def dh_call(d, w2, x, dy, gain, tn=256, parts=3):
+def dh_call(d, w2, x, dy, gain, tn=512, parts=3):
     nb, nk, seq, dc = d.shape
     nw, w, tw = w2.shape
     m = x.shape[0]
@@ -235,7 +235,7 @@
 TW = 2 * HD
 NCH = 4
 UT = 3
-SLOTS, RSLOTS = 4, 10
+SLOTS, RSLOTS = 3, 10
 CHUNK = 2
 MESH = pl.DeviceIdType.MESH
 
@@ -284,7 +284,7 @@
 
 def kg_kernel(nchip, owned, plan, h_own, dy_own, cs_own, wq, wk, wv, wo,
               h_all, dy_all, w2, a_own, a4, dqkv, cs_all, q_hbm, k_hbm, v_hbm, da_hbm, a_tmp,
-              lhs, rope,
+              lhs, rope, wt, wot,
               send, recv, csend, crecv, wsend, wrecv, rsend, rrecv, osend, orecv, asend, arecv, fsend, frecv,
               lsem, wsem, osem, isem, iosem, aisem, aosem, ownsem, bsem):
     nb, bt, width = h_own.shape
@@ -396,14 +396,17 @@
 
     def key_head(b, i): return me if b == owned else 2 * mine(i // 2) + i % 2
 
-    def tiles(t, pos_list, per, shape, start, wait, compute, dst, mid):
+    primed = set()
+
+    def tiles(t, pos_list, per, buf, start, wait, compute, dst, mid):
         b, kind = t // 2, t % 2
         m0, m = pos_list[0] * cb, len(pos_list) * cb
         cnt = per * (1 if b == owned else nloc)
         tid = lambda x: per * key_head(b, x // per) + x % per
 
-        def scope(buf, ost):
-            for x in range(min(cnt, SLOTS)): start(tid(x), buf, x)
+        def scope(ost):
+            prime(t)
+            primed.discard(t)
             for pos in pos_list:
                 for cp in loads(t, pos): cp.wait()
             if pos_list[0] == 0: own_back(t).start()
@@ -433,15 +436,15 @@
             lax.fori_loop(0, cnt, body, 0)
             for x in (cnt - 2, cnt - 1): stores(x, x % 2, False)
             if pos_list[0] == 0: own_back(t).wait()
-        pl.run_scoped(scope, V((SLOTS,) + shape, BF), V((2, m, TW), BF))
+        pl.run_scoped(scope, V((2, m, TW), BF))
 
     def run(cp, start_it): cp.start() if start_it else cp.wait()
 
     def w_start(n, buf, slot):
         c = width // NCH
-        for y in range(NCH): local(w2.at[n, pl.ds(y * c, c), :], buf.at[slot, pl.ds(y * c, c), :], wsem.at[slot]).start()
-
-    def w_wait(n, buf, slot): local(w2.at[n], buf.at[slot], wsem.at[slot]).wait()
+        for y in range(NCH): local(w2.at[n, pl.ds(y * c, c), :], buf.at[slot, pl.ds(y * c, c), :], wsem.at[0, slot]).start()
+
+    def w_wait(n, buf, slot): local(w2.at[n], buf.at[slot], wsem.at[0, slot]).wait()
 
     def qkv_dst(b, i, u, rr, src, slot, y, start_it):
         @pl.when(u < 2)
@@ -462,13 +465,13 @@
                 ost[slot, ro, 0:HD] = rot(res[rr, 0:HD], c, s).astype(BF)
                 ost[slot, ro, HD:TW] = jnp.where(u == 2, res[rr, HD:TW], rot(res[rr, HD:TW], c, s)).astype(BF)
 
-    def qkv(b, pos_list, mid={}): tiles(2 * b, pos_list, UT, (width, TW), w_start, w_wait, qkv_compute, qkv_dst, mid)
+    def qkv(b, pos_list, mid={}): tiles(2 * b, pos_list, UT, wt, w_start, w_wait, qkv_compute, qkv_dst, mid)
 
     def o_start(n, buf, slot):
         c = TW // NCH
-        for y in range(NCH): local(wo.at[ds(n * NCH + y, c), :], buf.at[slot, pl.ds(y * c, c), :], wsem.at[slot]).start()
-
-    def o_wait(n, buf, slot): local(wo.at[ds(n, TW), :], buf.at[slot], wsem.at[slot]).wait()
+        for y in range(NCH): local(wo.at[ds(n * NCH + y, c), :], buf.at[slot, pl.ds(y * c, c), :], wsem.at[1, slot]).start()
+
+    def o_wait(n, buf, slot): local(wo.at[ds(n, TW), :], buf.at[slot], wsem.at[1, slot]).wait()
 
     def da_dst(b, i, u, rr, src, slot, y, start_it): run(local(src, da_hbm.at[b, i, rr, ds(u, TW)], osem.at[slot, y]), start_it)
 
@@ -477,7 +480,13 @@
             n = min(CHUNK, len(pos_list) - y0) * cb
             ost[slot, y0 * cb:y0 * cb + n, :] = ntdot(left(y0 * cb, n), w[...]).astype(BF)
 
-    def da(b, pos_list, mid={}): tiles(2 * b + 1, pos_list, 2, (TW, width), o_start, o_wait, da_compute, da_dst, mid)
+    def da(b, pos_list, mid={}): tiles(2 * b + 1, pos_list, 2, wot, o_start, o_wait, da_compute, da_dst, mid)
+
+    def prime(t):
+        if t in primed: return
+        primed.add(t)
+        b, per, buf, start = t // 2, (UT, 2)[t % 2], (wt, wot)[t % 2], (w_start, o_start)[t % 2]
+        for x in range(min(per * (1 if b == owned else nloc), SLOTS)): start(per * key_head(b, x // per) + x % per, buf, x)
 
     OCT = nkv
 
@@ -631,7 +640,13 @@
 
     ACT = {'L0': lambda t, ps: [cp.start() for p in ps for cp in loads(t, p)], 'T': cs_send, 'TF': cs_forward, 'TR': cs_ready, 'D': lambda t: rings[t][0](), 'F': lambda t: rings[t][1](), 'G': lambda t: rings[t][2](), 'N': lambda t, ps: [rings[t][3](p) for p in ps],
            'L': load, 'RQ': rl_q, 'SQ': q_send, 'RK': rl_kv, 'WQ': wq_ready, 'WK': wkv_ready, 'Q': qkv, 'O': da, 'AS': a_send, 'IN': all_in, 'H': lambda b, j, ops: hooks.setdefault(b, {}).update({j: ops}), 'A': att}
-    for op, *ar in plan: ACT[op](*ar)
+    tensor = lambda op, b, *ar: 2 * b + (op == 'O')
+    for j, (op, *ar) in enumerate(plan):
+        if op in ('Q', 'O', 'A'):
+            later = [o for o in plan[j + 1:] if o[0] in ('Q', 'O')][:1]
+            for o in later:
+                if o[0] != op and (op == 'A' or o[:2] != ('Q', owned)): prime(tensor(*o))
+        ACT[op](*ar)
     for make, ar in pending: make(*ar).wait_send()
 
 
@@ -640,7 +655,7 @@
 PLAN = [('T', S0), ('D', S0), ('D', S1), ('T', S1), ('T', S2), ('RK', S0), ('RK', S1), ('RQ', S0), ('TF', S0), ('F', S0), ('D', S2), ('RQ', S1), ('TR', S0), ('L', S0, NEAR), ('WK',),
         ('Q', S0, NEAR, {S2: [('SQ', S0)], S6: [('F', S1), ('D', S3)], S10: [('L', S1, NEAR)]}), ('G', S0), ('L', S0, FAR), ('SQ', S1), ('O', S0, NEAR), ('TF', S1), ('TF', S2), ('Q', S0, FAR),
         ('F', S2), ('D', S4), ('G', S1), ('L', S1, FAR), ('TR', S1), ('TR', S2), ('L', S2, NEAR), ('O', S0, FAR),
-        ('H', S0, S1, [('F', S3), ('D', S5)]), ('H', S0, S2, [('L', S3, NEAR), ('G', S2), ('L', S2, FAR)]), ('A', S0), ('WQ',),
+        ('H', S0, S1, [('F', S3), ('D', S5)]), ('H', S0, S2, [('L', S3, NEAR), ('G', S2), ('L', S2, FAR)]), ('WQ',), ('A', S0),
         ('Q', S1, EACH), ('L', S4, HERE), ('F', S4), ('Q', S2, HERE), ('G', S3), ('L', S3, FAR), ('L', S4, NEAR[S1:]), ('O', S1, EACH), ('L', S5, HERE), ('A', S1),
         ('F', S5), ('D', S6), ('AS',), ('G', S4), ('L', S4, FAR), ('L', S5, NEAR[S1:]), ('Q', S2, AWAY, {S9: [('G', S5), ('L', S5, FAR)]}), ('O', S2, EACH), ('H', S2, S1, [('F', S6)]), ('H', S2, S3, [('G', S6)]), ('A', S2), ('N', S6, EACH), ('IN',)]
 RB = 128
@@ -655,8 +670,8 @@
     outs = [seqs(T, width)] * 2 + [sds((UT * nkv, width, TW), BF), seqs(nkv, bt, QW), seqs(T, QW), seqs(nkv, T, QW + TW), sds((nb, T, HD), F32),
             seqs(nloc, T, QW), seqs(nloc, T, HD), seqs(nloc, T, HD), seqs(nloc, T, QW), seqs(nloc, T, QW)]
     two = lambda *s: [DS(s), DS(s)]
-    scratch = [V((2, T, width), BF), V((nb, 2, T, HD), F32)] + two(2 * nb, 8) + two(nb, 7) + two(2 * NCH + nkv) + two(nb - 1, nloc, 2) + two(8) + two(ncp) + two(nb - 1)
-    scratch += [DS((2, 5)), DS((SLOTS,)), DS((2, 8)), DS((RSLOTS,)), DS((2, 8)), DS((2, 4)), DS((2, 4)), DS((2,)), DS((ncp,))]
+    scratch = [V((2, T, width), BF), V((nb, 2, T, HD), F32), V((SLOTS, width, TW), BF), V((SLOTS, TW, width), BF)] + two(2 * nb, 8) + two(nb, 7) + two(2 * NCH + nkv) + two(nb - 1, nloc, 2) + two(8) + two(ncp) + two(nb - 1)
+    scratch += [DS((2, 5)), DS((2, SLOTS)), DS((2, 8)), DS((RSLOTS,)), DS((2, 8)), DS((2, 4)), DS((2, 4)), DS((2,)), DS((ncp,))]
     return pl.pallas_call(functools.partial(kg_kernel, ncp // 2, owned, plan or PLAN), out_shape=outs, in_specs=[ANY] * 7, out_specs=[ANY] * len(outs), scratch_shapes=scratch,
                           compiler_params=params(collective_id=0, has_side_effects=True), name='gather')(h_own, dy_own, cs_own, wq, wk, wv, wo)
 

time: 558 us -> 540 us (0.968)
  Pallas kernels: 543 us -> 525 us
    pallas_call x1, Pallas kernels: 390 us -> 378 us  [kg_call(): pl.pallas_call(functools.partial(kg_kernel, ncp // 2, owned, plan or PLAN...]
where the time goes in v2:
time: 540 us; the launch traced here: 530 us
  Pallas kernels  525 us (97%)
    pallas_call x1, Pallas kernels, kg_call(): pl.pallas_call(functools.partial(kg_kernel, ncp // 2, owned, plan or PLAN...  378 us
    pallas_call x1, Pallas kernels, dh_call(): pl.pallas_call(functools.partial(dh_kernel, nt, parts), grid=(nt + 1,), i...  45.9 us
    pallas_call x1, Pallas kernels, dw_call(): pl.pallas_call(functools.partial(dw_kernel, 4), grid=(nq + 2,), in_specs=...  32.3 us
    pallas_call x1, Pallas kernels, out_call(): pl.pallas_call(functools.partial(out_kernel, parts), grid=(w // tn,), in_...  26.7 us
    pallas_call x1, Pallas kernels, dwo_call(): pl.pallas_call(functools.partial(dwo_kernel, parts), grid=(w // tn,), in_...  24.1 us
    pallas_call x1, Pallas kernels, sum_call(): pl.pallas_call(functools.partial(sum_kernel, ncp), in_specs=[full], out_s...  11.1 us

profile of v2, /device:TPU:113, one launch (start us, length us, event | category | flops | bytes accessed | tf_op | source)
XLA Modules:
  0.0 530.3 jit_solution(3791852224810668278)
XLA Ops:
  0.6 0.7 convert_element_type.3
  1.3 0.8 multiply_cosine_fusion
  2.1 0.9 pad_maximum_fusion.cs_own
  3.0 6.8 %norm.1 = bf16[384,5120]{1,0:T(8,128)(2,1)} custom-call(bf16[384,5120]{1,0:T(8,128)(2,1)} %bitcast.15, f32[1,5120]{1,0:T(1,128)} %bitcast.23, f32[1,5120]{1,0:T(1,128)} %bitcast.25), custom_call_target="tpu_custom_call" | custom-call | tf_op jit(solution)/shard_map/norm/pallas_call | solution.py:39
  9.8 378.4 %gather.1 = (bf16[3,1024,5120]{2,1,0:T(8,128)(2,1)}, bf16[3,1024,5120]{2,1,0:T(8,128)(2,1)}, bf16[24,5120,256]{2,1,0:T(8,128)(2,1)}, bf16[3,8,128,512]{3,2,1,0:T...) custom-call(bf16[3,128,5120]{2,1,0:T(8,128)(2,1)} %bitcast.19, ...), custom_call_target="tpu_custom_call" | custom-call | tf_op jit(solution)/shard_map/gather/pallas_call | solution.py:675
  388.2 26.7 %out.1 = bf16[384,5120]{1,0:T(8,128)(2,1)} custom-call(bf16[3,8,128,512]{3,2,1,0:T(8,128)(2,1)} %get-tuple-element.19.a_ref, bf16[4096,5120]{1,0:T(8,128)(2,1)} %refs_3_.1, bf16[4096,5120]{1,0:T(8,128)(2,1)} %refs_3_.1, bf16[4096,5120]{1,0:T(8,128)(2,1)} %refs_3_.1, bf16[4096,5120]{1,0:T(8,128)(2,1)} %refs_3_.1, bf16[384,5120]{1,0:T(8,128)(2,1)} %bitcast.16), custom_call_target="tpu_custom_call" | custom-call | tf_op jit(solution)/shard_map/out/pallas_call | solution.py:62
  414.9 45.9 %dh.1 = (bf16[384,5120]{1,0:T(8,128)(2,1)}, f32[16,5120]{1,0:T(8,128)}) custom-call(bf16[3,8,1024,768]{3,2,1,0:T(8,128)(2,1)} %get-tuple-element.20.d_ref, bf16[24,5120,256]{2,1,0:T(8,128)(2,1)} %get-tuple-element.21.refs_0_.refs_1_.refs_2_, bf16[24,5120,256]{2,1,0:T(8,128)(2,1)} %get-tuple-element.21.refs_0_.refs_1_.refs_2_, ...), custom_call_target="tpu_custom_call" | custom-call | tf_op jit(solution)/shard_map/dh/pallas_call | solution.py:202
  460.8 32.3 %dw.1 = (f32[640,32,128]{2,1,0:T(8,128)}, f32[640,8,128]{2,1,0:T(8,128)}, f32[640,8,128]{2,1,0:T(8,128)}) custom-call(bf16[3072,5120]{1,0:T(8,128)(2,1)} %bitcast.18, bf16[3,8,1024,768]{3,2,1,0:T(8,128)(2,1)} %get-tuple-element.20.d_ref), custom_call_target="tpu_custom_call" | custom-call | tf_op jit(solution)/shard_map/dw/pallas_call | solution.py:148
  493.1 11.1 %sums.1 = f32[2,5120]{1,0:T(2,128)} custom-call(f32[16,5120]{1,0:T(8,128)} %get-tuple-element.29.s_ref), custom_call_target="tpu_custom_call" | custom-call | tf_op jit(solution)/shard_map/sums/pallas_call | solution.py:227
  504.2 1.5 fusion.1
  505.7 24.1 %dwo.1 = f32[512,5120]{1,0:T(8,128)} custom-call(bf16[3072,512]{1,0:T(8,128)(2,1)} %bitcast.22, bf16[3072,5120]{1,0:T(8,128)(2,1)} %bitcast.12, bf16[3072,5120]{1,0:T(8,128)(2,1)} %bitcast.13, bf16[3072,5120]{1,0:T(8,128)(2,1)} %bitcast.14), custom_call_target="tpu_custom_call" | custom-call | tf_op jit(solution)/shard_map/dwo/pallas_call | solution.py:79
  (1 shorter events, 0.0 us)
